TPU v7x, 32 devices: a whole 2x2x4 slice. The times are simulated.
32 devices in a mesh: dp: 4 (over z), tensor: 8 (over y, x, core).
Axes of the slice: x: 2, y: 2, z: 4, core: 2. Of those that a mesh axis runs over, the one named last changes fastest.
Arguments:
- activations: bfloat16 [1024, 27648], P('dp', 'tensor'), may hold values from -6 to 6
- left_factor: float32 [216, 216], replicated, may hold values from -2 to 3, as said below
- right_factor: float32 [128, 128], replicated, may hold values from -2 to 3, as said below
- clip_scale: float32 [128, 216], replicated, may hold values from 0.5 to 3
- weight_rows: bfloat16 [27648, 5120], P('tensor'), may hold values from -0.0390625 to 0.0390625
- target: bfloat16 [1024, 5120], P('dp'), may hold values from -6 to 6
Outputs:
- grad_left: float32 [216, 216], replicated
- grad_right: float32 [128, 128], replicated
- grad_input: float32 [1024, 27648], P('dp', 'tensor')
Inputs may be any that keep to these rules, and one draw needn't show every extreme that they name: `left_factor`: the identity plus independent entries of order one over the square root of 216. `right_factor`: the identity plus independent entries of order one over the square root of 128.
All inputs are finite; a program needn't handle non-finite values.
Results may differ from a plain program's by a relative error of at most 0.007.
Values may be sent and summed in bfloat16 or wider, within the bound.
A program may use at most 128 MiB of HBM per device.

v0:
```python
import jax
import jax.numpy as jnp
from jax import lax
from jax.sharding import PartitionSpec as P


def local(activations, left_factor, right_factor, clip_scale, weight_rows, target):
    highest = lax.Precision.HIGHEST
    tok_rows = activations.shape[0]
    width_left = left_factor.shape[0]
    local_right = activations.shape[1] // width_left
    inputs = activations.reshape(tok_rows, local_right, width_left)
    moved = lax.all_to_all(inputs, "tensor", split_axis=0, concat_axis=1, tiled=True)
    mixed = jnp.einsum("tji,ik->tjk", moved.astype(jnp.float32), left_factor, precision=highest)
    rotated = jnp.einsum("jl,tjk->tlk", right_factor, mixed, precision=highest)
    bounded = jnp.tanh(rotated / clip_scale)
    clipped = (clip_scale * bounded).astype(jnp.bfloat16)
    clipped_back = lax.all_to_all(clipped, "tensor", split_axis=1, concat_axis=0, tiled=True)
    partial_out = jnp.dot(
        clipped_back.reshape(tok_rows, -1), weight_rows, preferred_element_type=jnp.float32
    )
    total = lax.psum(partial_out, "tensor")
    out_grad = (total - target.astype(jnp.float32)).astype(jnp.bfloat16)
    clipped_grad = lax.dot_general(
        out_grad, weight_rows, (((1,), (1,)), ((), ())), preferred_element_type=jnp.float32
    )
    clipped_grad = clipped_grad.reshape(tok_rows, local_right, width_left)
    grad_owned = lax.all_to_all(clipped_grad, "tensor", split_axis=0, concat_axis=1, tiled=True)
    rotated_grad = grad_owned * (1.0 - bounded * bounded)
    mixed_grad = jnp.einsum("jl,tlk->tjk", right_factor, rotated_grad, precision=highest)
    right_part = jnp.einsum("tjk,tlk->jl", mixed, rotated_grad, precision=highest)
    grad_back = lax.all_to_all(mixed_grad, "tensor", split_axis=1, concat_axis=0, tiled=True)
    input_grad = jnp.einsum("tjk,ik->tji", grad_back, left_factor, precision=highest).reshape(
        tok_rows, -1
    )
    left_part = jnp.einsum("tji,tjk->ik", inputs.astype(jnp.float32), grad_back, precision=highest)
    left_sum, right_sum = lax.psum((left_part, right_part), ("dp", "tensor"))
    return (left_sum, right_sum, input_grad)


def solution(mesh):
    placed = (P("dp", "tensor"), P(), P(), P(), P("tensor", None), P("dp", None))
    return jax.shard_map(
        local, mesh=mesh, in_specs=placed, out_specs=(P(), P(), P("dp", "tensor")), check_vma=False
    )
```

profile of v0, /device:TPU:8, one launch (start us, length us, event | category | flops | bytes accessed | tf_op | source)
XLA Modules:
  0.0 508.3 jit_solution(451690624203319944)
XLA Ops:
  7.2 0.0 all-reduce.4.cloned.1.call-start
  7.2 2.7 copy.31
  9.9 3.0 copy.32
  12.9 30.3 %all_to_all.69 = bf16[256,16,216]{2,1,0:T(8,128)(2,1)S(1)} all-to-all(bf16[256,16,216]{2,1,0:T(8,128)(2,1)} %copy.32), channel_id=1, replica_groups=mesh['dp'=4,'tensor'=8] {'tensor'}, dimensions={0} | all-to-all | bytes 3538944 | tf_op jit(solution)/shard_map/all_to_all | solution.py:13
  43.2 0.3 copy.33
  43.5 2.1 fusion.6
  45.7 4.7 multiply_convert_fusion
  50.4 4.5 copy.36
  54.9 30.1 %all_to_all.70 = bf16[32,128,216]{2,0,1:T(8,128)(2,1)S(1)} all-to-all(bf16[32,128,216]{2,0,1:T(8,128)(2,1)} %copy.36), channel_id=1, replica_groups=mesh['dp'=4,'tensor'=8] {'tensor'}, dimensions={1} | all-to-all | bytes 3538944 | tf_op jit(solution)/shard_map/all_to_all | solution.py:18
  85.0 2.6 copy.38
  87.6 5.2 %reshape.21 = bf16[256,3456]{1,0:T(8,128)(2,1)} reshape(bf16[8,32,16,216]{3,2,1,0:T(8,128)(2,1)} %copy.38) | data formatting | bytes 3538944 | tf_op jit(solution)/shard_map/reshape | solution.py:20
  92.8 18.0 %fusion.12 = f32[256,5120]{1,0:T(8,128)} fusion(bf16[256,3456]{1,0:T(8,128)(2,1)} %reshape.21, bf16[3456,5120]{1,0:T(8,128)(2,1)} %param.10), kind=kOutput, calls=%fused_computation.18 | convolution fusion | flops 9059696640 | bytes 42401792 | tf_op jit(solution)/shard_map/dot_general | solution.py:19
  110.8 91.8 %all-reduce.4.cloned.1.call-done = f32[256,5120]{1,0:T(8,128)} async-done(((f32[256,5120]{1,0:T(8,128)}), f32[256,5120]{1,0:T(8,128)}) %all-reduce.4.cloned.1.call-update) | async-done | bytes 5242896 | tf_op jit(solution)/shard_map/psum | solution.py:22
  202.6 19.4 %fusion.1 = f32[256,3456]{0,1:T(8,128)} fusion(bf16[3456,5120]{1,0:T(8,128)(2,1)} %param.10, f32[256,5120]{1,0:T(8,128)} %all-reduce.4.cloned.1.call-done, bf16[256,5120]{1,0:T(8,128)(2,1)} %param.11), kind=kOutput, calls=%fused_computation.5 | convolution fusion | flops 9063628800 | bytes 46792704 | tf_op jit(solution)/shard_map/dot_general | solution.py:24
  222.0 5.3 %copy.40 = f32[256,16,216]{2,1,0:T(8,128)} copy(f32[256,16,216]{0,2,1:T(8,128)} %bitcast.63) | data formatting | bytes 7077888 | tf_op jit(solution)/shard_map/reshape | solution.py:27
  227.3 52.6 %all_to_all.71 = f32[256,16,216]{2,1,0:T(8,128)S(1)} all-to-all(f32[256,16,216]{2,1,0:T(8,128)} %copy.40), channel_id=1, replica_groups=mesh['dp'=4,'tensor'=8] {'tensor'}, dimensions={0} | all-to-all | bytes 7077888 | tf_op jit(solution)/shard_map/all_to_all | solution.py:28
  279.9 2.7 copy.41
  282.6 5.5 %copy.42 = f32[32,128,216]{1,2,0:T(8,128)} copy(f32[32,128,216]{2,1,0:T(8,128)} %bitcast.55) | data formatting | bytes 7077888 | tf_op jit(solution)/shard_map/all_to_all | solution.py:28
  288.1 6.4 %convolution_bitcast_fusion = f32[32,128,216]{1,2,0:T(8,128)} fusion(f32[32,128,216]{1,2,0:T(8,128)} %copy.42, f32[32,128,216]{1,2,0:T(8,128)} %get-tuple-element.15, f32[128,128]{1,0:T(8,128)S(1)} %copy-done.2), kind=kOutput, calls=%fused_computation.6 | convolution fusion | flops 1361608704 | bytes 10682368 | tf_op jit(solution)/shard_map/jl,tlk->tjk/dot_general | solution.py:30
  294.5 5.3 %copy.43 = f32[32,128,216]{2,0,1:T(8,128)} copy(f32[32,128,216]{1,2,0:T(8,128)} %convolution_bitcast_fusion) | data formatting | bytes 7077888 | tf_op jit(solution)/shard_map/jl,tlk->tjk/transpose | solution.py:30
  299.7 4.6 all-to-all-start.3
  304.3 0.3 all-reduce.6.cloned.1.call-start
  304.5 10.7 %fusion.3 = f32[128,128]{1,0:T(8,128)} fusion(f32[32,128,216]{1,2,0:T(8,128)} %copy-done.1, f32[32,128,216]{1,2,0:T(8,128)} %copy.42, f32[32,128,216]{1,2,0:T(8,128)} %get-tuple-element.15), kind=kOutput, calls=%fused_computation.9 | convolution fusion | flops 1361608704 | bytes 10682368 | tf_op jit(solution)/shard_map/tjk,tlk->jl/dot_general | solution.py:31
  315.3 38.1 %all-to-all-done.3 = f32[32,128,216]{2,0,1:T(8,128)} async-done(((f32[32,128,216]{2,0,1:T(8,128)}), f32[32,128,216]{2,0,1:T(8,128)}, u32[]{:S(2)}, u32[]{:S(2)}) %all-to-all-start.3) | async-done | bytes 3538976 | tf_op jit(solution)/shard_map/all_to_all | solution.py:32
  353.4 6.5 %copy.45 = f32[8,32,16,216]{3,2,1,0:T(8,128)} copy(f32[8,32,16,216]{3,1,2,0:T(8,128)} %bitcast.17) | data formatting | bytes 7077888 | tf_op jit(solution)/shard_map/all_to_all | solution.py:32
  359.9 5.1 %copy.46 = f32[256,16,216]{0,2,1:T(8,128)} copy(f32[256,16,216]{2,1,0:T(8,128)} %bitcast.56) | data formatting | bytes 7077888 | tf_op jit(solution)/shard_map/all_to_all | solution.py:32
  365.0 4.6 convolution_bitcast_fusion.1
  369.6 7.1 %fusion.4 = f32[256,16,216]{0,2,1:T(8,128)} fusion(f32[256,16,216]{0,2,1:T(8,128)} %copy.46, f32[216,216]{1,0:T(8,128)S(1)} %copy-done), kind=kOutput, calls=%fused_computation.10 | convolution fusion | flops 2293235712 | bytes 7264512 | tf_op jit(solution)/shard_map/tjk,ik->tji/dot_general | solution.py:33
  376.7 5.2 %copy.49 = f32[256,3456]{1,0:T(8,128)} copy(f32[256,3456]{0,1:T(8,128)} %bitcast.59) | data formatting | bytes 7077888
  381.9 116.3 %all-reduce.6.cloned.1.call-done = (f32[216,216]{0,1:T(8,128)}, f32[128,128]{1,0:T(8,128)}) async-done(((f32[216,216]{0,1:T(8,128)}, f32[128,128]{1,0:T(8,128)}), (f32[216,216]{0,1:T(8,128)}, f32[128,128]{1,0:T(8,128)})) %all-reduce.6.cloned.1.call-update) | async-done | bytes 252176 | tf_op jit(solution)/shard_map/psum | solution.py:37
  498.2 1.7 copy.48
  499.9 1.5 copy.59
  (10 shorter events, 0.1 us)
Async XLA Ops:
  7.2 36.4 %copy-start = (f32[216,216]{1,0:T(8,128)S(1)}, f32[216,216]{1,0:T(8,128)}, u32[]{:S(2)}) copy-start(f32[216,216]{1,0:T(8,128)} %param.7) | copy-start | bytes 559876
  7.2 195.4 %all-reduce.4.cloned.1.call-start = ((), (), s32[]{:S(2)}) async-start(), calls=%async_computation.4 | async-start | bytes 10485760 | tf_op jit(solution)/shard_map/psum | solution.py:22
  43.5 2.2 copy-start.2
  43.5 2.2 copy-start.3
  45.7 4.7 copy-start.1
  299.7 53.7 %all-to-all-start.3 = ((f32[32,128,216]{2,0,1:T(8,128)}), f32[32,128,216]{2,0,1:T(8,128)}, u32[]{:S(2)}, u32[]{:S(2)}) async-start(f32[32,128,216]{2,0,1:T(8,128)} %copy.43), calls=%async_computation.3 | async-start | bytes 8388608 | tf_op jit(solution)/shard_map/all_to_all | solution.py:32
  304.3 193.9 %all-reduce.6.cloned.1.call-start = ((), (), s32[]{:S(2)}) async-start(), calls=%async_computation.5 | async-start | bytes 573440 | tf_op jit(solution)/shard_map/psum | solution.py:37
Sparse Core Ops, SparseCore 0:
  110.9 91.6 all-reduce.3
  369.7 128.4 all-reduce.5
where the time goes:
time: 510 us; the launch traced here: 508 us
  waiting for transfers between devices  246 us (48%)
  blocking collectives  113 us (22%)
  matrix products  72.9 us (14%)
  local copies, waits for them, and re-layouts  57 us (11%)
  between operations  14.1 us (3%)
    psum x1, waiting for transfers between devices, local(): left_sum, right_sum = lax.psum((left_part, right_part), ('dp', 'tensor'))  116 us
    psum x1, waiting for transfers between devices, local(): total = lax.psum(partial_out, 'tensor')  91.8 us
    all_to_all x1, blocking collectives, local(): lax.all_to_all(clipped_grad, 'tensor', split_axis=0, concat_axis=1, tiled...  52.6 us
    all_to_all x1, waiting for transfers between devices, local(): lax.all_to_all(mixed_grad, 'tensor', split_axis=1, concat_axis=0, tiled=T...  38.1 us
    all_to_all x1, blocking collectives, local(): lax.all_to_all(inputs, 'tensor', split_axis=0, concat_axis=1, tiled=True)  30.3 us
    all_to_all x1, blocking collectives, local(): lax.all_to_all(clipped, 'tensor', split_axis=1, concat_axis=0, tiled=True)  30.1 us
    dot_general x1, matrix products, local(): lax.dot_general(out_grad, weight_rows, (((1,), (1,)), ((), ())), preferre...  19.4 us
    dot_general x1, matrix products, local(): jnp.dot(clipped_back.reshape(tok_rows, -1), weight_rows, preferred_elemen...  18 us
  transfers between devices with their start and end apart: 3, of which 3 were waited for; matrix products, arithmetic and copies ran while one was open for 5% of the time, Pallas kernels for 0%

commit v1 on v0

v1 whole, which is shorter than its diff:
```python
import jax
import jax.numpy as jnp
from jax import lax
from jax.experimental import pallas as pl
from jax.experimental.pallas import tpu as pltpu
from jax.sharding import PartitionSpec as P

BF = jnp.bfloat16
F32 = jnp.float32


def finish_kernel(grad_ref, act_ref, factor_ref, out_ref, left_ref):
    order = factor_ref.shape[0]
    factor = factor_ref[...]

    @pl.when(pl.program_id(0) == 0)
    def _():
        left_ref[...] = jnp.zeros_like(left_ref)

    total = jnp.zeros((order, order), F32)
    for j in range(grad_ref.shape[1] // order):
        here = slice(j * order, (j + 1) * order)
        grad = grad_ref[:, here]
        out_ref[:, here] = lax.dot_general(
            grad, factor, (((1,), (1,)), ((), ())), preferred_element_type=F32
        )
        total = total + lax.dot_general(
            act_ref[:, here], grad, (((0,), (0,)), ((), ())), preferred_element_type=F32
        )
    left_ref[...] += total


def finish(grad, act, factor):
    rows, width = grad.shape
    order = factor.shape[0]
    tile = min(rows, 128)
    return pl.pallas_call(
        finish_kernel,
        grid=(rows // tile,),
        in_specs=[
            pl.BlockSpec((tile, width), lambda i: (i, 0)),
            pl.BlockSpec((tile, width), lambda i: (i, 0)),
            pl.BlockSpec((order, order), lambda i: (0, 0)),
        ],
        out_specs=[
            pl.BlockSpec((tile, width), lambda i: (i, 0)),
            pl.BlockSpec((order, order), lambda i: (0, 0)),
        ],
        out_shape=[
            jax.ShapeDtypeStruct((rows, width), F32),
            jax.ShapeDtypeStruct((order, order), F32),
        ],
        compiler_params=pltpu.CompilerParams(vmem_limit_bytes=48 * 1024 * 1024),
        cost_estimate=pl.CostEstimate(
            flops=4 * rows * width * order, bytes_accessed=8 * rows * width, transcendentals=0
        ),
    )(grad, act, factor.astype(BF))


def split(value):
    head = value.astype(BF)
    return head, (value - head.astype(F32)).astype(BF)


def dot(a, b, dims):
    return lax.dot_general(a, b, ((dims[:1], dims[1:]), ((), ())), preferred_element_type=F32)


def forward_kernel(
    act_ref, left_ref, right_ref, clip_ref, out_ref, mixed_ref, bounded_ref, rows_ref, cols_ref
):
    peers, own, width = act_ref.shape
    order = left_ref.shape[0]
    each = width // order
    left_hi, left_lo = split(left_ref[...])
    right_hi, right_lo = split(right_ref[...])
    clip = clip_ref[...]

    @pl.loop(0, peers)
    def _(s):
        x = jnp.concatenate(
            [act_ref[s, :, j * order : (j + 1) * order] for j in range(each)], axis=0
        )
        mixed = dot(x, left_hi, (1, 0)) + dot(x, left_lo, (1, 0))
        for j in range(each):
            rows_ref[s * each + j] = mixed[j * own : (j + 1) * own]

    @pl.loop(0, own, unroll=4)
    def _(t):
        mixed = rows_ref[:, t, :]
        hi, lo = split(mixed)
        mixed_ref[t] = hi
        rotated = (
            dot(right_hi, hi, (0, 0)) + dot(right_lo, hi, (0, 0)) + dot(right_hi, lo, (0, 0))
        )
        bounded = jnp.tanh(rotated / clip)
        bounded_ref[t] = bounded
        cols_ref[:, t, :] = clip * bounded

    @pl.loop(0, peers)
    def _(s):
        for j in range(each):
            out_ref[s, :, j * order : (j + 1) * order] = cols_ref[s * each + j].astype(BF)


def backward_kernel(
    grad_ref, mixed_ref, bounded_ref, right_ref, out_ref, sum_ref, rows_ref, cols_ref
):
    peers, own, width = grad_ref.shape
    order = bounded_ref.shape[2]
    each = width // order
    right = right_ref[...].astype(BF)

    @pl.loop(0, peers)
    def _(s):
        for j in range(each):
            rows_ref[s * each + j] = grad_ref[s, :, j * order : (j + 1) * order].astype(F32)

    sum_ref[...] = jnp.zeros_like(sum_ref)

    @pl.loop(0, own, unroll=4)
    def _(t):
        bounded = bounded_ref[t]
        rotated_grad = (rows_ref[:, t, :] * (1.0 - bounded * bounded)).astype(BF)
        sum_ref[...] += dot(mixed_ref[t], rotated_grad, (1, 1))
        cols_ref[:, t, :] = dot(right, rotated_grad, (1, 0))

    @pl.loop(0, peers)
    def _(s):
        for j in range(each):
            out_ref[s, :, j * order : (j + 1) * order] = cols_ref[s * each + j].astype(BF)


def owner_call(kernel, outs, scratch, *args):
    return pl.pallas_call(
        kernel,
        out_shape=[jax.ShapeDtypeStruct(*out) for out in outs],
        in_specs=[pl.BlockSpec(memory_space=pltpu.VMEM)] * len(args),
        out_specs=[pl.BlockSpec(memory_space=pltpu.VMEM)] * len(outs),
        scratch_shapes=[pltpu.VMEM(scratch, F32)] * 2,
        compiler_params=pltpu.CompilerParams(vmem_limit_bytes=56 * 1024 * 1024),
    )(*args)


def local(activations, left_factor, right_factor, clip_scale, weight_rows, target):
    peers = lax.axis_size("tensor")
    everyone = lax.axis_size("dp") * peers
    tok_rows, width = activations.shape
    width_left = left_factor.shape[0]
    width_right = right_factor.shape[0]
    own = tok_rows // peers

    def exchange(blocks):
        got = lax.all_to_all(
            blocks.reshape(tok_rows, width), "tensor", split_axis=0, concat_axis=0, tiled=True
        )
        return got.reshape(peers, own, width)

    flat = (peers, own, width)
    cube = (own, width_right, width_left)
    by_row = (width_right, own, width_left)
    clipped, mixed, bounded = owner_call(
        forward_kernel, [(flat, BF), (cube, BF), (cube, F32)], by_row,
        exchange(activations), left_factor, right_factor, clip_scale,
    )
    clipped = exchange(clipped).reshape(tok_rows, width)
    partial_out = jnp.dot(clipped, weight_rows, preferred_element_type=F32).astype(BF)
    chips = peers // 2
    core = lax.axis_index("tensor") % 2
    same_core = [[2 * q + c for q in range(chips)] for c in range(2)]
    swap = [(d, d ^ 1) for d in range(peers)]
    blocks = partial_out.reshape(chips, 2, own, -1)
    there = lax.dynamic_index_in_dim(blocks, 1 - core, 1, keepdims=False)
    here = lax.dynamic_index_in_dim(blocks, core, 1, keepdims=False)
    there = lax.ppermute(there, "tensor", swap)
    paired = (here.astype(F32) + there.astype(F32)).astype(BF)
    terms = lax.all_to_all(
        paired, "tensor", split_axis=0, concat_axis=0, axis_index_groups=same_core, tiled=True
    )
    total = jnp.sum(terms.astype(F32), axis=0)
    mine = lax.dynamic_slice_in_dim(target, lax.axis_index("tensor") * own, own, 0)
    mine = (total - mine.astype(F32)).astype(BF)
    got = lax.all_to_all(
        jnp.broadcast_to(mine[None], (chips, *mine.shape)),
        "tensor", split_axis=0, concat_axis=0, axis_index_groups=same_core, tiled=True,
    )
    other = lax.ppermute(got, "tensor", swap)
    first = jnp.where(core == 0, got, other)
    second = jnp.where(core == 0, other, got)
    out_grad = jnp.stack([first, second], axis=1).reshape(tok_rows, -1)
    clipped_grad = lax.dot_general(
        out_grad, weight_rows, (((1,), (1,)), ((), ())), preferred_element_type=F32
    ).astype(BF)
    mixed_grad, right_part = owner_call(
        backward_kernel, [(flat, BF), ((width_right, width_right), F32)], by_row,
        exchange(clipped_grad), mixed, bounded, right_factor,
    )
    grad_back = exchange(mixed_grad).reshape(tok_rows, width)
    input_grad, left_part = finish(grad_back, activations, left_factor)

    cols = max(width_left, width_right)
    stacked = jnp.concatenate(
        [
            jnp.pad(left_part, ((0, 0), (0, cols - width_left))),
            jnp.pad(right_part, ((0, 0), (0, cols - width_right))),
        ],
        axis=0,
    )
    rows = -(-stacked.shape[0] // (8 * peers)) * 8
    stacked = jnp.pad(stacked, ((0, rows * peers - stacked.shape[0]), (0, 0)))

    def spread(piece, axis, times):
        copies = jnp.broadcast_to(piece[None], (times, *piece.shape))
        return lax.all_to_all(copies, axis, split_axis=0, concat_axis=0, tiled=True)

    shares = lax.all_to_all(
        stacked.reshape(peers, rows, cols), "tensor", split_axis=0, concat_axis=0, tiled=True
    )
    share = jnp.sum(spread(jnp.sum(shares, axis=0), "dp", lax.axis_size("dp")), axis=0)
    sums = spread(share, "tensor", peers).reshape(rows * peers, cols)
    left_sum = sums[:width_left, :width_left]
    right_sum = sums[width_left : width_left + width_right, :width_right]
    return (left_sum, right_sum, input_grad)


def solution(mesh):
    placed = (P("dp", "tensor"), P(), P(), P(), P("tensor", None), P("dp", None))
    return jax.shard_map(
        local, mesh=mesh, in_specs=placed, out_specs=(P(), P(), P("dp", "tensor")), check_vma=False
    )
```

time: 510 us -> 280 us (0.55)
  waiting for transfers between devices: 246 us -> 90 us
  local copies, waits for them, and re-layouts: 57 us -> 6.86 us
  Pallas kernels: 0 us -> 46.4 us
  matrix products: 72.9 us -> 32.9 us
  blocking collectives: 113 us -> 78.7 us
  between operations: 14.1 us -> 0.77 us
  starting transfers between devices: 4.85 us -> 14.9 us
  other arithmetic: 0 us -> 6.02 us
    psum x2 -> x0, waiting for transfers between devices: 208 us -> none  [the longest x1 116 us: local(): left_sum, right_sum = lax.psum((left_part, right_part), ('dp', 'tensor'))]
    pallas_call x0 -> x3, Pallas kernels: none -> 46.4 us  [the longest x2 37.5 us: owner_call(): pl.pallas_call(kernel, out_shape=[jax.ShapeDtypeStruct(*out) for out in o...]
    all_to_all x1 -> x4, waiting for transfers between devices: 38.1 us -> 83.6 us  [the longest x3 66.6 us: exchange(): lax.all_to_all(blocks.reshape(tok_rows, width), 'tensor', split_axis=0, c...]
    dot_general x7 -> x1, matrix products: 53.6 us -> 16.5 us  [local(): jnp.dot(clipped, weight_rows, preferred_element_type=F32).astype(BF)]
    all_to_all x3 -> x5, blocking collectives: 113 us -> 78.7 us  [the longest x1 27.4 us: exchange(): lax.all_to_all(blocks.reshape(tok_rows, width), 'tensor', split_axis=0, c...]
    all_to_all x6 -> x0, local copies, waits for them, and re-layouts: 22.7 us -> none  [the longest x2 11.7 us: local(): lax.all_to_all(mixed_grad, 'tensor', split_axis=1, concat_axis=0, tiled=T...]
    reshape x3 -> x0, local copies, waits for them, and re-layouts: 13.5 us -> none  [the longest x1 5.3 us: local(): clipped_grad = clipped_grad.reshape(tok_rows, local_right, width_left)]
    all_to_all x1 -> x4, starting transfers between devices: 4.55 us -> 14.9 us  [the longest x3 11.4 us: exchange(): lax.all_to_all(blocks.reshape(tok_rows, width), 'tensor', split_axis=0, c...]
  transfers between devices with their start and end apart: 3 -> 6, of which waited for: 3 -> 6; matrix products, arithmetic and copies ran while one was open for 5% -> 1% of each run, Pallas kernels for 0% -> 0%
where the time goes in v1:
time: 280 us; the launch traced here: 277 us
  waiting for transfers between devices  90 us (32%)
  blocking collectives  78.7 us (28%)
  Pallas kernels  46.4 us (17%)
  matrix products  32.9 us (12%)
  starting transfers between devices  14.9 us (5%)
  local copies, waits for them, and re-layouts  6.86 us (2%)
  other arithmetic  6.02 us (2%)
    all_to_all x3, waiting for transfers between devices, exchange(): lax.all_to_all(blocks.reshape(tok_rows, width), 'tensor', split_axis=0, c...  66.6 us
    pallas_call x2, Pallas kernels, owner_call(): pl.pallas_call(kernel, out_shape=[jax.ShapeDtypeStruct(*out) for out in o...  37.5 us
    all_to_all x1, blocking collectives, exchange(): lax.all_to_all(blocks.reshape(tok_rows, width), 'tensor', split_axis=0, c...  27.4 us
    all_to_all x2, blocking collectives, spread(): return lax.all_to_all(copies, axis, split_axis=0, concat_axis=0, tiled=True)  21.6 us
    all_to_all x1, blocking collectives, local(): lax.all_to_all(jnp.broadcast_to(mine[None], (chips, *mine.shape)), 'tenso...  19.1 us
    all_to_all x1, waiting for transfers between devices, local(): lax.all_to_all(paired, 'tensor', split_axis=0, concat_axis=0, axis_index_...  17 us
    dot_general x1, matrix products, local(): jnp.dot(clipped, weight_rows, preferred_element_type=F32).astype(BF)  16.5 us
    dot_general x1, matrix products, local(): lax.dot_general(out_grad, weight_rows, (((1,), (1,)), ((), ())), preferre...  16.4 us
  transfers between devices with their start and end apart: 6, of which 6 were waited for; matrix products, arithmetic and copies ran while one was open for 1% of the time, Pallas kernels for 0%

profile of v1, /device:TPU:8, one launch (start us, length us, event | category | flops | bytes accessed | tf_op | source)
XLA Modules:
  0.0 276.5 jit_solution(11222155936612393815)
XLA Ops:
  0.6 3.9 %all-to-all-start = ((bf16[8,32,3456]{2,1,0:T(8,128)(2,1)}), bf16[8,32,3456]{2,1,0:T(8,128)(2,1)S(1)}, u32[]{:S(2)}, u32[]{:S(2)}) async-start(bf16[8,32,3456]{2,1,0:T(8,128)(2,1)} %bitcast.23), calls=%async_computation | async-start | bytes 3538944 | tf_op jit(solution)/shard_map/all_to_all | solution.py:154
  4.5 0.8 copy.12.clip_ref
  5.3 22.3 %all-to-all-done.act_ref = bf16[8,32,3456]{2,1,0:T(8,128)(2,1)S(1)} async-done(((bf16[8,32,3456]{2,1,0:T(8,128)(2,1)}), bf16[8,32,3456]{2,1,0:T(8,128)(2,1)S(1)}, u32[]{:S(2)}, u32[]{:S(2)}) %all-to-all-start) | async-done | bytes 1769504 | tf_op jit(solution)/shard_map/all_to_all | solution.py:154
  27.6 1.2 copy-done.2
  28.9 25.3 %shard_map.85 = (bf16[8,32,3456]{2,1,0:T(8,128)(2,1)}, bf16[32,128,216]{2,1,0:T(8,128)(2,1)}, f32[32,128,216]{2,1,0:T(8,128)}) custom-call(bf16[8,32,3456]{2,1,0:T(8,128)(2,1)} %copy-done.2, f32[216,216]{1,0:T(8,128)} %left_ref.1, f32[128,128]{1,0:T(8,128)} %right_ref.3, f32[128,216]{1,0:T(8,128)} %copy.12.clip_ref), custom_call_target="tpu_custom_call" | custom-call | tf_op jit(solution)/shard_map/pallas_call | solution.py:135
  54.1 3.6 %all-to-all-start.1 = ((bf16[8,32,3456]{2,1,0:T(8,128)(2,1)}), bf16[8,32,3456]{2,1,0:T(8,128)(2,1)S(1)}, u32[]{:S(2)}, u32[]{:S(2)}) async-start(bf16[8,32,3456]{2,1,0:T(8,128)(2,1)} %get-tuple-element.10), calls=%async_computation.1 | async-start | bytes 3538944 | tf_op jit(solution)/shard_map/all_to_all | solution.py:154
  57.7 23.0 %all-to-all-done.1 = bf16[8,32,3456]{2,1,0:T(8,128)(2,1)S(1)} async-done(((bf16[8,32,3456]{2,1,0:T(8,128)(2,1)}), bf16[8,32,3456]{2,1,0:T(8,128)(2,1)S(1)}, u32[]{:S(2)}, u32[]{:S(2)}) %all-to-all-start.1) | async-done | bytes 1769504 | tf_op jit(solution)/shard_map/all_to_all | solution.py:154
  80.8 1.2 copy-done.3
  82.0 16.5 %convolution_convert_fusion = bf16[256,5120]{1,0:T(8,128)(2,1)S(1)} fusion(bf16[256,3456]{1,0:T(8,128)(2,1)} %bitcast.28, bf16[3456,5120]{1,0:T(8,128)(2,1)} %param.10), kind=kOutput, calls=%fused_computation | convolution fusion | flops 9061007360 | bytes 39780352 | tf_op jit(solution)/shard_map/dot_general | solution.py:167
  98.5 1.2 dynamic-slice_bitcast_fusion
  99.7 3.4 %collective-permute-done = bf16[4,32,5120]{2,1,0:T(8,128)(2,1)} collective-permute-done((bf16[4,32,5120]{2,1,0:T(8,128)(2,1)}, bf16[4,32,5120]{2,1,0:T(8,128)(2,1)}, u32[]{:S(2)}, u32[]{:S(2)}) %collective-permute-start) | collective-permute-done | bytes 1310752 | tf_op jit(solution)/shard_map/ppermute | solution.py:175
  103.1 2.7 fusion
  105.8 3.5 %all-to-all-start.2 = ((bf16[4,32,5120]{2,1,0:T(8,128)(2,1)}), bf16[4,32,5120]{2,1,0:T(8,128)(2,1)S(1)}, u32[]{:S(2)}, u32[]{:S(2)}) async-start(bf16[4,32,5120]{2,1,0:T(8,128)(2,1)} %fusion), calls=%async_computation.2 | async-start | bytes 2621440 | tf_op jit(solution)/shard_map/all_to_all | solution.py:177
  109.3 17.0 %all-to-all-done.2 = bf16[4,32,5120]{2,1,0:T(8,128)(2,1)S(1)} async-done(((bf16[4,32,5120]{2,1,0:T(8,128)(2,1)}), bf16[4,32,5120]{2,1,0:T(8,128)(2,1)S(1)}, u32[]{:S(2)}, u32[]{:S(2)}) %all-to-all-start.2) | async-done | bytes 1310752 | tf_op jit(solution)/shard_map/all_to_all | solution.py:177
  126.3 0.2 convert_reduce_fusion
  126.5 1.1 subtract_convert_fusion
  127.7 19.1 %all_to_all.60 = bf16[4,32,5120]{2,1,0:T(8,128)(2,1)S(1)} all-to-all(bf16[4,32,5120]{2,1,0:T(8,128)(2,1)S(1)} %broadcast_in_dim.6), channel_id=1, replica_groups={{0,2,4,6},{1,3,5,7},{8,10,12,14},{9,11,13,15},{16,18,20,22},{17,19,21,2..., dimensions={0} | all-to-all | bytes 2621440 | tf_op jit(solution)/shard_map/all_to_all | solution.py:183
  146.8 3.0 %collective-permute-done.1 = bf16[4,32,5120]{2,1,0:T(8,128)(2,1)S(1)} collective-permute-done((bf16[4,32,5120]{2,1,0:T(8,128)(2,1)S(1)}, bf16[4,32,5120]{2,1,0:T(8,128)(2,1)S(1)}, u32[]{:S(2)}, u32[]{:S(2)}) %collective-permute-start.1) | collective-permute-done | bytes 1310752 | tf_op jit(solution)/shard_map/ppermute | solution.py:187
  150.0 0.2 pad_maximum_fusion
  150.2 16.4 %convolution_convert_fusion.1 = bf16[256,3456]{1,0:T(8,128)(2,1)} fusion(bf16[256,5120]{1,0:T(8,128)(2,1)S(1)} %bitcast.27, bf16[3456,5120]{1,0:T(8,128)(2,1)} %param.10), kind=kOutput, calls=%fused_computation.1 | convolution fusion | flops 9060581376 | bytes 39780352 | tf_op jit(solution)/shard_map/dot_general | solution.py:191
  166.6 27.4 %all_to_all.61.grad_ref = bf16[8,32,3456]{2,1,0:T(8,128)(2,1)} all-to-all(bf16[8,32,3456]{2,1,0:T(8,128)(2,1)} %bitcast.29), channel_id=1, replica_groups=mesh['dp'=4,'tensor'=8] {'tensor'}, dimensions={0} | all-to-all | bytes 3538944 | tf_op jit(solution)/shard_map/all_to_all | solution.py:154
  194.0 12.2 %shard_map.86 = (bf16[8,32,3456]{2,1,0:T(8,128)(2,1)}, f32[128,128]{1,0:T(8,128)}) custom-call(bf16[8,32,3456]{2,1,0:T(8,128)(2,1)} %all_to_all.61.grad_ref, bf16[32,128,216]{2,1,0:T(8,128)(2,1)} %get-tuple-element.11.mixed_ref, f32[32,128,216]{2,1,0:T(8,128)} %get-tuple-element.12.bounded_ref, f32[128,128]{1,0:T(8,128)} %right_ref.3), custom_call_target="tpu_custom_call" | custom-call | tf_op jit(solution)/shard_map/pallas_call | solution.py:135
  206.2 3.9 %all-to-all-start.5 = ((bf16[8,32,3456]{2,1,0:T(8,128)(2,1)}), bf16[8,32,3456]{2,1,0:T(8,128)(2,1)S(1)}, u32[]{:S(2)}, u32[]{:S(2)}) async-start(bf16[8,32,3456]{2,1,0:T(8,128)(2,1)} %get-tuple-element.13), calls=%async_computation.5 | async-start | bytes 3538944 | tf_op jit(solution)/shard_map/all_to_all | solution.py:154
  210.1 1.6 convert_element_type.43.factor_ref
  211.7 21.3 %all-to-all-done.5 = bf16[8,32,3456]{2,1,0:T(8,128)(2,1)S(1)} async-done(((bf16[8,32,3456]{2,1,0:T(8,128)(2,1)}), bf16[8,32,3456]{2,1,0:T(8,128)(2,1)S(1)}, u32[]{:S(2)}, u32[]{:S(2)}) %all-to-all-start.5) | async-done | bytes 1769504 | tf_op jit(solution)/shard_map/all_to_all | solution.py:154
  233.0 0.9 copy-done.1
  233.9 8.9 %shard_map.87 = (f32[256,3456]{1,0:T(8,128)}, f32[216,216]{1,0:T(8,128)S(1)}) custom-call(bf16[256,3456]{1,0:T(8,128)(2,1)S(1)} %bitcast.24, bf16[256,3456]{1,0:T(8,128)(2,1)S(1)} %copy-done, bf16[216,216]{1,0:T(8,128)(2,1)S(1)} %copy-done.1), custom_call_target="tpu_custom_call" | custom-call | flops 764411904 | bytes 7077888 | tf_op jit(solution)/shard_map/pallas_call | solution.py:37
  242.8 10.7 %all_to_all.62 = f32[8,48,216]{2,1,0:T(8,128)S(1)} all-to-all(f32[8,48,216]{2,1,0:T(8,128)S(1)} %bitcast.30), channel_id=1, replica_groups=mesh['dp'=4,'tensor'=8] {'tensor'}, dimensions={0} | all-to-all | bytes 663552 | tf_op jit(solution)/shard_map/all_to_all | solution.py:216
  253.6 10.9 %all_to_all.63 = f32[4,48,216]{2,1,0:T(8,128)S(1)} all-to-all(f32[4,48,216]{2,1,0:T(8,128)S(1)} %broadcast_in_dim.7), channel_id=1, replica_groups=mesh['dp'=4,'tensor'=8] {'dp'}, dimensions={0} | all-to-all | bytes 331776 | tf_op jit(solution)/shard_map/all_to_all | solution.py:214
  264.5 10.7 %all_to_all.64 = f32[8,48,216]{2,1,0:T(8,128)S(1)} all-to-all(f32[8,48,216]{2,1,0:T(8,128)S(1)} %broadcast_in_dim.8), channel_id=1, replica_groups=mesh['dp'=4,'tensor'=8] {'tensor'}, dimensions={0} | all-to-all | bytes 663552 | tf_op jit(solution)/shard_map/all_to_all | solution.py:214
  275.2 0.7 slice.8
  275.9 0.6 slice.9
  (19 shorter events, 0.5 us)
Async XLA Ops:
  0.6 3.9 %copy-start.4 = (f32[128,216]{0,1:T(8,128)S(1)}, f32[128,216]{0,1:T(8,128)}, u32[]{:S(2)}) copy-start(f32[128,216]{0,1:T(8,128)} %param.9) | copy-start | bytes 331780
  0.6 27.0 %all-to-all-start = ((bf16[8,32,3456]{2,1,0:T(8,128)(2,1)}), bf16[8,32,3456]{2,1,0:T(8,128)(2,1)S(1)}, u32[]{:S(2)}, u32[]{:S(2)}) async-start(bf16[8,32,3456]{2,1,0:T(8,128)(2,1)} %bitcast.23), calls=%async_computation | async-start | bytes 3538944 | tf_op jit(solution)/shard_map/all_to_all | solution.py:154
  27.6 1.2 copy-start.2
  54.1 26.6 %all-to-all-start.1 = ((bf16[8,32,3456]{2,1,0:T(8,128)(2,1)}), bf16[8,32,3456]{2,1,0:T(8,128)(2,1)S(1)}, u32[]{:S(2)}, u32[]{:S(2)}) async-start(bf16[8,32,3456]{2,1,0:T(8,128)(2,1)} %get-tuple-element.10), calls=%async_computation.1 | async-start | bytes 3538944 | tf_op jit(solution)/shard_map/all_to_all | solution.py:154
  80.8 1.2 copy-start.3
  99.7 3.4 %collective-permute-start = (bf16[4,32,5120]{2,1,0:T(8,128)(2,1)}, bf16[4,32,5120]{2,1,0:T(8,128)(2,1)}, u32[]{:S(2)}, u32[]{:S(2)}) collective-permute-start(bf16[4,32,5120]{2,1,0:T(8,128)(2,1)} %dynamic-slice_bitcast_fusion), channel_id=1, source_target_pairs={{0,1},{1,0},{2,3},{3,2},{4,5},{5,4},{6,7},{7,6},{8,9},{9,8},{10,11... | collective-permute-start | bytes 3932168 | tf_op jit(solution)/shard_map/ppermute | solution.py:175
  105.8 20.5 %all-to-all-start.2 = ((bf16[4,32,5120]{2,1,0:T(8,128)(2,1)}), bf16[4,32,5120]{2,1,0:T(8,128)(2,1)S(1)}, u32[]{:S(2)}, u32[]{:S(2)}) async-start(bf16[4,32,5120]{2,1,0:T(8,128)(2,1)} %fusion), calls=%async_computation.2 | async-start | bytes 2621440 | tf_op jit(solution)/shard_map/all_to_all | solution.py:177
  146.8 3.0 %collective-permute-start.1 = (bf16[4,32,5120]{2,1,0:T(8,128)(2,1)S(1)}, bf16[4,32,5120]{2,1,0:T(8,128)(2,1)S(1)}, u32[]{:S(2)}, u32[]{:S(2)}) collective-permute-start(bf16[4,32,5120]{2,1,0:T(8,128)(2,1)S(1)} %all_to_all.60), channel_id=1, source_target_pairs={{0,1},{1,0},{2,3},{3,2},{4,5},{5,4},{6,7},{7,6},{8,9},{9,8},{10,11... | collective-permute-start | bytes 3932168 | tf_op jit(solution)/shard_map/ppermute | solution.py:187
  206.2 26.8 %copy-start = (bf16[256,3456]{1,0:T(8,128)(2,1)S(1)}, bf16[256,3456]{1,0:T(8,128)(2,1)}, u32[]{:S(2)}) copy-start(bf16[256,3456]{1,0:T(8,128)(2,1)} %act_ref.1) | copy-start | bytes 5308420
  206.2 26.8 %all-to-all-start.5 = ((bf16[8,32,3456]{2,1,0:T(8,128)(2,1)}), bf16[8,32,3456]{2,1,0:T(8,128)(2,1)S(1)}, u32[]{:S(2)}, u32[]{:S(2)}) async-start(bf16[8,32,3456]{2,1,0:T(8,128)(2,1)} %get-tuple-element.13), calls=%async_computation.5 | async-start | bytes 3538944 | tf_op jit(solution)/shard_map/all_to_all | solution.py:154
  233.0 0.9 copy-start.1
  233.9 8.9 %copy-start.5 = (f32[128,128]{1,0:T(8,128)S(1)}, f32[128,128]{1,0:T(8,128)}, u32[]{:S(2)}) copy-start(f32[128,128]{1,0:T(8,128)} %get-tuple-element.15) | copy-start | bytes 196612
